TPU v7x, 32 devices: a whole 2x2x4 slice. The times are simulated.
32 devices in a mesh: expert: 4 (over x, core), shard: 8 (over z, y).
Axes of the slice: x: 2, y: 2, z: 4, core: 2. Of those that a mesh axis runs over, the one named last changes fastest.
Arguments:
- tokens: bfloat16 [48, 4096], P('shard', 'expert'), may hold values from -6 to 6
- expert_ids: int32 [48, 2], P('shard'), may hold values from 0 to 3, all different within a row; in each aligned block of 6 rows (0 to 5, 6 to 11, ...) at most 6 rows name the same one
- gates: float32 [48, 2], P('shard'), may hold values from 0.1 to 1
- gate_proj: bfloat16 [4, 4096, 8192], P('expert', None, 'shard'), may hold values from -0.09375 to 0.09375
- up_proj: bfloat16 [4, 4096, 8192], P('expert', None, 'shard'), may hold values from -0.09375 to 0.09375
- down_proj_t: bfloat16 [4, 4096, 8192], P('expert', 'shard'), may hold values from -0.0625 to 0.0625
Outputs:
- mixed: bfloat16 [48, 4096], P('shard', 'expert')
Inputs may be any that keep to these rules, and one draw needn't show every extreme that they name: `expert_ids`: each token names two different experts; among the 6 tokens of one aligned block no expert is named more than 6 times, and in every draw some expert is named exactly 6 times in some block.
All inputs are finite; a program needn't handle non-finite values.
Results may differ from a plain program's by a relative error of at most 0.0085.
Values may be sent and summed in bfloat16 or wider, within the bound.
A program may use at most 64 MiB of HBM per device.

v0:
```python
import jax
import jax.numpy as jnp
from jax import lax
from jax.sharding import PartitionSpec as P


def shards(tokens, expert_ids, gates, gate_proj, up_proj, down_proj_t):
    experts = lax.axis_size("expert")
    own_expert = lax.axis_index("expert")
    tok_count = tokens.shape[0]
    capacity = min(tok_count, 4 * tok_count // experts)
    expert_range = jnp.arange(experts, dtype=jnp.int32)
    matches = expert_ids[:, :, None] == expert_range[None, None, :]
    routed = jnp.sum(matches.astype(jnp.int32), axis=1)
    weight = jnp.sum(gates[:, :, None] * matches.astype(jnp.float32), axis=1)
    slot_rank = jnp.cumsum(routed, axis=0) - routed
    slot_range = jnp.arange(capacity, dtype=jnp.int32)
    selector = (slot_rank.T[:, None, :] == slot_range[None, :, None]) & (routed.T[:, None, :] > 0)
    selector_bf = selector.astype(jnp.bfloat16)
    whole = lax.all_gather(tokens, "expert", axis=1, tiled=True)
    own_select = lax.dynamic_index_in_dim(selector_bf, own_expert, 0, keepdims=False)
    own_rows = jnp.dot(own_select, whole, preferred_element_type=jnp.float32).astype(jnp.bfloat16)
    gate_local = gate_proj[0]
    up_local = up_proj[0]
    down_local = down_proj_t[0]
    piece = lax.all_gather(own_rows, "shard", axis=0, tiled=True)
    gate_out = jnp.dot(piece, gate_local, preferred_element_type=jnp.float32)
    up_out = jnp.dot(piece, up_local, preferred_element_type=jnp.float32)
    hidden = (jax.nn.silu(gate_out) * up_out).astype(jnp.bfloat16)
    out_columns = lax.dot_general(
        lax.all_gather(hidden, "shard", axis=1, tiled=True),
        down_local,
        (((1,), (1,)), ((), ())),
        preferred_element_type=jnp.float32,
    )
    expert_out = lax.all_to_all(
        out_columns.astype(jnp.bfloat16), "shard", split_axis=0, concat_axis=1, tiled=True
    )
    gathered_out = lax.all_to_all(expert_out, "expert", split_axis=1, concat_axis=0, tiled=True)
    combiner = (
        (selector.astype(jnp.float32) * weight.T[:, None, :])
        .reshape(experts * capacity, tok_count)
        .T
    )
    mixed_sum = jnp.dot(combiner, gathered_out.astype(jnp.float32), precision=lax.Precision.HIGHEST)
    return mixed_sum.astype(jnp.bfloat16)


def solution(mesh):
    in_specs = (
        P("shard", "expert"),
        P("shard", None),
        P("shard", None),
        P("expert", None, "shard"),
        P("expert", None, "shard"),
        P("expert", "shard", None),
    )
    out_specs = P("shard", "expert")
    return jax.shard_map(shards, mesh=mesh, in_specs=in_specs, out_specs=out_specs, check_vma=False)
```

profile of v0, /device:TPU:0, one launch (start us, length us, event | category | flops | bytes accessed | tf_op | source)
XLA Modules:
  0.0 105.6 jit_solution(6960518200582428909)
XLA Ops:
  0.0 0.7 convert_reduce_fusion
  0.7 0.2 reduce_window_sum.11
  0.9 6.4 %all_gather.9 = bf16[6,4096]{1,0:T(8,128)(2,1)S(1)} all-gather(bf16[6,1024]{1,0:T(8,128)(2,1)} %param.6), channel_id=1, replica_groups=mesh['expert'=4,'shard'=8] {'expert'}, dimensions={1}, use_global_device_ids=true | all-gather | bytes 61440 | tf_op jit(solution)/shard_map/all_gather | solution.py:20
  7.3 0.1 fusion.6
  7.5 32.4 %all-gather = bf16[8,6,4096]{2,1,0:T(8,128)(2,1)S(1)} all-gather(bf16[1,6,4096]{2,1,0:T(8,128)(2,1)S(1)} %fusion.6), channel_id=1, replica_groups=mesh['expert'=4,'shard'=8] {'shard'}, dimensions={0}, use_global_device_ids=true | all-gather | bytes 442368 | tf_op jit(solution)/shard_map/all_gather | solution.py:26
  39.9 0.1 reshape.15
  40.0 0.0 slice-start
  40.0 5.1 %fusion.4 = f32[48,1024]{1,0:T(8,128)S(1)} fusion(bf16[48,4096]{1,0:T(8,128)(2,1)S(1)} %reshape.15, bf16[1,4096,1024]{2,1,0:T(8,128)(2,1)} %param.9), kind=kOutput, calls=%fused_computation.4 | convolution fusion | flops 402653184 | bytes 8978432 | tf_op jit(solution)/shard_map/dot_general | solution.py:27
  45.1 0.0 slice-start.1
  45.1 5.1 %fusion.10 = bf16[48,1024]{1,0:T(8,128)(2,1)S(1)} fusion(bf16[48,4096]{1,0:T(8,128)(2,1)S(1)} %reshape.15, bf16[1,4096,1024]{2,1,0:T(8,128)(2,1)} %param.10, f32[48,1024]{1,0:T(8,128)S(1)} %fusion.4), kind=kOutput, calls=%fused_computation.9 | convolution fusion | flops 402948096 | bytes 9076736 | tf_op jit(solution)/shard_map/dot_general | solution.py:28
  50.2 0.0 copy-start
  50.3 0.0 copy-start.1
  50.3 31.6 %all_gather.11 = bf16[48,8192]{1,0:T(8,128)(2,1)S(1)} all-gather(bf16[48,1024]{1,0:T(8,128)(2,1)S(1)} %fusion.10), channel_id=1, replica_groups=mesh['expert'=4,'shard'=8] {'shard'}, dimensions={1}, use_global_device_ids=true | all-gather | bytes 884736 | tf_op jit(solution)/shard_map/all_gather | solution.py:31
  81.9 0.0 slice-done
  81.9 0.0 slice-done.1
  81.9 2.6 %fusion.13 = bf16[48,512]{1,0:T(8,128)(2,1)S(1)} fusion(bf16[48,8192]{1,0:T(8,128)(2,1)S(1)} %all_gather.11, bf16[1,512,8192]{2,1,0:T(8,128)(2,1)S(1)} %bitcast.40), kind=kOutput, calls=%fused_computation.10 | convolution fusion | flops 402677760 | bytes 9224192 | tf_op jit(solution)/shard_map/dot_general | solution.py:30
  84.6 12.8 %all_to_all.32 = bf16[8,6,512]{2,1,0:T(8,128)(2,1)} all-to-all(bf16[8,6,512]{2,1,0:T(8,128)(2,1)S(1)} %all_to_all.24), channel_id=1, replica_groups=mesh['expert'=4,'shard'=8] {'shard'}, dimensions={0} | all-to-all | bytes 98304 | tf_op jit(solution)/shard_map/all_to_all | solution.py:36
  97.4 3.3 %all-to-all-start.1 = ((bf16[6,4,1024]{2,0,1:T(8,128)(2,1)}), bf16[6,4,1024]{2,0,1:T(8,128)(2,1)S(1)}, u32[]{:S(2)}, u32[]{:S(2)}) async-start(bf16[6,4,1024]{2,0,1:T(8,128)(2,1)} %bitcast.9), calls=%async_computation.1 | async-start | bytes 131072 | tf_op jit(solution)/shard_map/all_to_all | solution.py:39
  100.7 0.0 copy-done
  100.7 0.0 copy-done.1
  100.7 4.1 %all-to-all-done.1 = bf16[6,4,1024]{2,0,1:T(8,128)(2,1)S(1)} async-done(((bf16[6,4,1024]{2,0,1:T(8,128)(2,1)}), bf16[6,4,1024]{2,0,1:T(8,128)(2,1)S(1)}, u32[]{:S(2)}, u32[]{:S(2)}) %all-to-all-start.1) | async-done | bytes 49184 | tf_op jit(solution)/shard_map/all_to_all | solution.py:39
  104.8 0.8 fusion.16
  (6 shorter events, 0.1 us)
Async XLA Ops:
  40.0 41.9 %slice-start = ((s8[8388608]{0:T(1024)(128)(4,1)}), s8[4194304]{0:T(1024)(128)(4,1)S(1)}, s32[]{:S(2)}) async-start(s8[8388608]{0:T(1024)(128)(4,1)} %bitcast.39), calls=%async_computation.2 | async-start | bytes 8388608
  45.1 36.8 %slice-start.1 = ((s8[8388608]{0:T(1024)(128)(4,1)}), s8[4194304]{0:T(1024)(128)(4,1)S(1)}, s32[]{:S(2)}) async-start(s8[8388608]{0:T(1024)(128)(4,1)} %bitcast.39), calls=%async_computation.3 | async-start | bytes 8388608
  50.2 50.4 %copy-start = (s32[6,2]{0,1:T(2,128)S(1)}, s32[6,2]{0,1:T(2,128)}, u32[]{:S(2)}) copy-start(s32[6,2]{0,1:T(2,128)} %param.7) | copy-start | bytes 148
  50.3 50.4 %copy-start.1 = (f32[6,2]{0,1:T(2,128)S(1)}, f32[6,2]{0,1:T(2,128)}, u32[]{:S(2)}) copy-start(f32[6,2]{0,1:T(2,128)} %param.8) | copy-start | bytes 148
  97.4 7.4 %all-to-all-start.1 = ((bf16[6,4,1024]{2,0,1:T(8,128)(2,1)}), bf16[6,4,1024]{2,0,1:T(8,128)(2,1)S(1)}, u32[]{:S(2)}, u32[]{:S(2)}) async-start(bf16[6,4,1024]{2,0,1:T(8,128)(2,1)} %bitcast.9), calls=%async_computation.1 | async-start | bytes 131072 | tf_op jit(solution)/shard_map/all_to_all | solution.py:39
where the time goes:
time: 106 us
  blocking collectives  83.2 us (78%)
  matrix products  13.8 us (13%)
  waiting for transfers between devices  4.05 us (4%)
  starting transfers between devices  3.28 us (3%)
    all_gather x1, blocking collectives, shards(): piece = lax.all_gather(own_rows, 'shard', axis=0, tiled=True)  32.4 us
    all_gather x1, blocking collectives, shards(): lax.all_gather(hidden, 'shard', axis=1, tiled=True)  31.6 us
    all_to_all x1, blocking collectives, shards(): lax.all_to_all(out_columns.astype(jnp.bfloat16), 'shard', split_axis=0, c...  12.8 us
    all_gather x1, blocking collectives, shards(): whole = lax.all_gather(tokens, 'expert', axis=1, tiled=True)  6.44 us
    dot_general x1, matrix products, shards(): up_out = jnp.dot(piece, up_local, preferred_element_type=jnp.float32)  5.11 us
    dot_general x1, matrix products, shards(): gate_out = jnp.dot(piece, gate_local, preferred_element_type=jnp.float32)  5.1 us
    all_to_all x1, waiting for transfers between devices, shards(): lax.all_to_all(expert_out, 'expert', split_axis=1, concat_axis=0, tiled=T...  4.05 us
    all_to_all x1, starting transfers between devices, shards(): lax.all_to_all(expert_out, 'expert', split_axis=1, concat_axis=0, tiled=T...  3.28 us
  transfers between devices with their start and end apart: 1, of which 1 were waited for; matrix products, arithmetic and copies ran while one was open for 0% of the time, Pallas kernels for 0%

commit v1 on v0

--- a/solution.py
+++ b/solution.py
@@ -17,7 +17,14 @@
     slot_range = jnp.arange(capacity, dtype=jnp.int32)
     selector = (slot_rank.T[:, None, :] == slot_range[None, :, None]) & (routed.T[:, None, :] > 0)
     selector_bf = selector.astype(jnp.bfloat16)
-    whole = lax.all_gather(tokens, "expert", axis=1, tiled=True)
+    ring = [tokens]
+    for hop in range(3):
+        ring.append(lax.ppermute(ring[-1], "expert", [(dev, (dev + 1) % 4) for dev in range(4)]))
+    whole = jnp.roll(
+        jnp.concatenate(ring[::-1], axis=1),
+        (lax.axis_index("expert") + 1) * ring[0].shape[1],
+        axis=1,
+    )
     own_select = lax.dynamic_index_in_dim(selector_bf, own_expert, 0, keepdims=False)
     own_rows = jnp.dot(own_select, whole, preferred_element_type=jnp.float32).astype(jnp.bfloat16)
     gate_local = gate_proj[0]

time: 106 us -> 111 us (1.047)
  waiting for transfers between devices: 4.05 us -> 12.8 us
  blocking collectives: 83.2 us -> 76.8 us
  local copies, waits for them, and re-layouts: 0.18 us -> 1.64 us
    ppermute x0 -> x3, waiting for transfers between devices: none -> 8.7 us  [shards(): lax.ppermute(ring[-1], 'expert', [(dev, (dev + 1) % 4) for dev in range(4)])]
    all_gather x1 -> x0, blocking collectives: 6.44 us -> none  [shards(): whole = lax.all_gather(tokens, 'expert', axis=1, tiled=True)]
  transfers between devices with their start and end apart: 1 -> 4, of which waited for: 1 -> 4; matrix products, arithmetic and copies ran while one was open for 0% -> 1% of each run, Pallas kernels for 0% -> 0%
where the time goes in v1:
time: 111 us; the launch traced here: 110 us
  blocking collectives  76.8 us (69%)
  matrix products  13.8 us (12%)
  waiting for transfers between devices  12.8 us (12%)
  starting transfers between devices  4.03 us (4%)
  local copies, waits for them, and re-layouts  1.64 us (1%)
    all_gather x1, blocking collectives, shards(): piece = lax.all_gather(own_rows, 'shard', axis=0, tiled=True)  32.6 us
    all_gather x1, blocking collectives, shards(): lax.all_gather(hidden, 'shard', axis=1, tiled=True)  31.7 us
    all_to_all x1, blocking collectives, shards(): lax.all_to_all(out_columns.astype(jnp.bfloat16), 'shard', split_axis=0, c...  12.5 us
    ppermute x3, waiting for transfers between devices, shards(): lax.ppermute(ring[-1], 'expert', [(dev, (dev + 1) % 4) for dev in range(4)])  8.7 us
    dot_general x1, matrix products, shards(): up_out = jnp.dot(piece, up_local, preferred_element_type=jnp.float32)  5.11 us
    dot_general x1, matrix products, shards(): gate_out = jnp.dot(piece, gate_local, preferred_element_type=jnp.float32)  5.1 us
    all_to_all x1, waiting for transfers between devices, shards(): lax.all_to_all(expert_out, 'expert', split_axis=1, concat_axis=0, tiled=T...  4.05 us
    all_to_all x1, starting transfers between devices, shards(): lax.all_to_all(expert_out, 'expert', split_axis=1, concat_axis=0, tiled=T...  3.28 us
  transfers between devices with their start and end apart: 4, of which 4 were waited for; matrix products, arithmetic and copies ran while one was open for 1% of the time, Pallas kernels for 0%

profile of v1, /device:TPU:0, one launch (start us, length us, event | category | flops | bytes accessed | tf_op | source)
XLA Modules:
  0.0 110.1 jit_solution(1243386473050031063)
XLA Ops:
  0.0 0.5 collective-permute-start
  0.5 0.7 convert_reduce_fusion
  1.2 0.2 reduce_window_sum.11
  1.4 2.7 %collective-permute-done = bf16[6,1024]{1,0:T(8,128)(2,1)S(1)} collective-permute-done((bf16[6,1024]{1,0:T(8,128)(2,1)}, bf16[6,1024]{1,0:T(8,128)(2,1)S(1)}, u32[]{:S(2)}, u32[]{:S(2)}) %collective-permute-start) | collective-permute-done | bytes 12320 | tf_op jit(solution)/shard_map/ppermute | solution.py:22
  4.0 0.1 collective-permute-start.1
  4.2 3.0 %collective-permute-done.1 = bf16[6,1024]{1,0:T(8,128)(2,1)S(1)} collective-permute-done((bf16[6,1024]{1,0:T(8,128)(2,1)S(1)}, bf16[6,1024]{1,0:T(8,128)(2,1)S(1)}, u32[]{:S(2)}, u32[]{:S(2)}) %collective-permute-start.1) | collective-permute-done | bytes 12320 | tf_op jit(solution)/shard_map/ppermute | solution.py:22
  7.2 0.1 collective-permute-start.2
  7.4 3.0 %collective-permute-done.2 = bf16[6,1024]{1,0:T(8,128)(2,1)S(1)} collective-permute-done((bf16[6,1024]{1,0:T(8,128)(2,1)S(1)}, bf16[6,1024]{1,0:T(8,128)(2,1)S(1)}, u32[]{:S(2)}, u32[]{:S(2)}) %collective-permute-start.2) | collective-permute-done | bytes 12320 | tf_op jit(solution)/shard_map/ppermute | solution.py:22
  10.4 0.7 constant_dynamic-update-slice_fusion.4
  11.1 0.7 constant_dynamic-update-slice_fusion
  11.8 0.1 fusion.6
  12.0 32.6 %all-gather = bf16[8,6,4096]{2,1,0:T(8,128)(2,1)S(1)} all-gather(bf16[1,6,4096]{2,1,0:T(8,128)(2,1)S(1)} %fusion.6), channel_id=1, replica_groups=mesh['expert'=4,'shard'=8] {'shard'}, dimensions={0}, use_global_device_ids=true | all-gather | bytes 442368 | tf_op jit(solution)/shard_map/all_gather | solution.py:33
  44.6 0.1 reshape.15
  44.7 0.0 slice-start
  44.7 5.1 %fusion.4 = f32[48,1024]{1,0:T(8,128)S(1)} fusion(bf16[48,4096]{1,0:T(8,128)(2,1)S(1)} %reshape.15, bf16[1,4096,1024]{2,1,0:T(8,128)(2,1)} %param.9), kind=kOutput, calls=%fused_computation.4 | convolution fusion | flops 402653184 | bytes 8978432 | tf_op jit(solution)/shard_map/dot_general | solution.py:34
  49.8 0.0 slice-start.1
  49.9 5.1 %fusion.10 = bf16[48,1024]{1,0:T(8,128)(2,1)S(1)} fusion(bf16[48,4096]{1,0:T(8,128)(2,1)S(1)} %reshape.15, bf16[1,4096,1024]{2,1,0:T(8,128)(2,1)} %param.10, f32[48,1024]{1,0:T(8,128)S(1)} %fusion.4), kind=kOutput, calls=%fused_computation.9 | convolution fusion | flops 402948096 | bytes 9076736 | tf_op jit(solution)/shard_map/dot_general | solution.py:35
  55.0 0.0 copy-start.1
  55.0 31.7 %all_gather.7 = bf16[48,8192]{1,0:T(8,128)(2,1)S(1)} all-gather(bf16[48,1024]{1,0:T(8,128)(2,1)S(1)} %fusion.10), channel_id=1, replica_groups=mesh['expert'=4,'shard'=8] {'shard'}, dimensions={1}, use_global_device_ids=true | all-gather | bytes 884736 | tf_op jit(solution)/shard_map/all_gather | solution.py:38
  86.7 2.6 %fusion.13 = bf16[48,512]{1,0:T(8,128)(2,1)S(1)} fusion(bf16[48,8192]{1,0:T(8,128)(2,1)S(1)} %all_gather.7, bf16[1,512,8192]{2,1,0:T(8,128)(2,1)S(1)} %bitcast.39), kind=kOutput, calls=%fused_computation.10 | convolution fusion | flops 402677760 | bytes 9224192 | tf_op jit(solution)/shard_map/dot_general | solution.py:37
  89.4 12.5 %all_to_all.32 = bf16[8,6,512]{2,1,0:T(8,128)(2,1)} all-to-all(bf16[8,6,512]{2,1,0:T(8,128)(2,1)S(1)} %all_to_all.24), channel_id=1, replica_groups=mesh['expert'=4,'shard'=8] {'shard'}, dimensions={0} | all-to-all | bytes 98304 | tf_op jit(solution)/shard_map/all_to_all | solution.py:43
  101.9 3.3 %all-to-all-start.1 = ((bf16[6,4,1024]{2,0,1:T(8,128)(2,1)}), bf16[6,4,1024]{2,0,1:T(8,128)(2,1)S(1)}, u32[]{:S(2)}, u32[]{:S(2)}) async-start(bf16[6,4,1024]{2,0,1:T(8,128)(2,1)} %bitcast.9), calls=%async_computation.1 | async-start | bytes 131072 | tf_op jit(solution)/shard_map/all_to_all | solution.py:46
  105.2 4.1 %all-to-all-done.1 = bf16[6,4,1024]{2,0,1:T(8,128)(2,1)S(1)} async-done(((bf16[6,4,1024]{2,0,1:T(8,128)(2,1)}), bf16[6,4,1024]{2,0,1:T(8,128)(2,1)S(1)}, u32[]{:S(2)}, u32[]{:S(2)}) %all-to-all-start.1) | async-done | bytes 49184 | tf_op jit(solution)/shard_map/all_to_all | solution.py:46
  109.3 0.8 fusion.16
  (17 shorter events, 0.1 us)
Async XLA Ops:
  0.0 4.0 %collective-permute-start = (bf16[6,1024]{1,0:T(8,128)(2,1)}, bf16[6,1024]{1,0:T(8,128)(2,1)S(1)}, u32[]{:S(2)}, u32[]{:S(2)}) collective-permute-start(bf16[6,1024]{1,0:T(8,128)(2,1)} %param.6), channel_id=1, source_target_pairs={{0,8},{8,16},{16,24},{24,0},{1,9},{9,17},{17,25},{25,1},{2,10},{10... | collective-permute-start | bytes 36872 | tf_op jit(solution)/shard_map/ppermute | solution.py:22
  4.0 3.2 %collective-permute-start.1 = (bf16[6,1024]{1,0:T(8,128)(2,1)S(1)}, bf16[6,1024]{1,0:T(8,128)(2,1)S(1)}, u32[]{:S(2)}, u32[]{:S(2)}) collective-permute-start(bf16[6,1024]{1,0:T(8,128)(2,1)S(1)} %collective-permute-done), channel_id=1, source_target_pairs={{0,8},{8,16},{16,24},{24,0},{1,9},{9,17},{17,25},{25,1},{2,10},{10... | collective-permute-start | bytes 36872 | tf_op jit(solution)/shard_map/ppermute | solution.py:22
  7.2 3.2 %collective-permute-start.2 = (bf16[6,1024]{1,0:T(8,128)(2,1)S(1)}, bf16[6,1024]{1,0:T(8,128)(2,1)S(1)}, u32[]{:S(2)}, u32[]{:S(2)}) collective-permute-start(bf16[6,1024]{1,0:T(8,128)(2,1)S(1)} %collective-permute-done.1), channel_id=1, source_target_pairs={{0,8},{8,16},{16,24},{24,0},{1,9},{9,17},{17,25},{25,1},{2,10},{10... | collective-permute-start | bytes 36872 | tf_op jit(solution)/shard_map/ppermute | solution.py:22
  44.7 42.0 %slice-start = ((s8[8388608]{0:T(1024)(128)(4,1)}), s8[4194304]{0:T(1024)(128)(4,1)S(1)}, s32[]{:S(2)}) async-start(s8[8388608]{0:T(1024)(128)(4,1)} %bitcast.38), calls=%async_computation.2 | async-start | bytes 8388608
  49.8 36.9 %slice-start.1 = ((s8[8388608]{0:T(1024)(128)(4,1)}), s8[4194304]{0:T(1024)(128)(4,1)S(1)}, s32[]{:S(2)}) async-start(s8[8388608]{0:T(1024)(128)(4,1)} %bitcast.38), calls=%async_computation.3 | async-start | bytes 8388608
  55.0 50.2 %copy-start = (s32[6,2]{0,1:T(2,128)S(1)}, s32[6,2]{0,1:T(2,128)}, u32[]{:S(2)}) copy-start(s32[6,2]{0,1:T(2,128)} %param.7) | copy-start | bytes 148
  55.0 50.2 %copy-start.1 = (f32[6,2]{0,1:T(2,128)S(1)}, f32[6,2]{0,1:T(2,128)}, u32[]{:S(2)}) copy-start(f32[6,2]{0,1:T(2,128)} %param.8) | copy-start | bytes 148
  101.9 7.4 %all-to-all-start.1 = ((bf16[6,4,1024]{2,0,1:T(8,128)(2,1)}), bf16[6,4,1024]{2,0,1:T(8,128)(2,1)S(1)}, u32[]{:S(2)}, u32[]{:S(2)}) async-start(bf16[6,4,1024]{2,0,1:T(8,128)(2,1)} %bitcast.9), calls=%async_computation.1 | async-start | bytes 131072 | tf_op jit(solution)/shard_map/all_to_all | solution.py:46
